TPU v7x, 32 devices: a whole 2x2x4 slice. The times are simulated.
32 devices in a mesh: replica: 2 (over x), tp: 8 (over z, y), sub: 2 (over core).
Axes of the slice: x: 2, y: 2, z: 4, core: 2. Of those that a mesh axis runs over, the one named last changes fastest.
Arguments:
- hidden_in: bfloat16 [8, 8192], P('replica'), parts along dimension 0, may hold values from -6 to 6
- norm_gain: float32 [16384], P('replica'), parts along dimension 0, may hold values from 0.1 to 1.9
- wqkv_old: bfloat16 [16, 2, 1280, 4096], P(('replica', 'tp'), 'sub'), parts along dimension 0, may hold values from -0.1875 to 0.1875
- wo: bfloat16 [16384, 8192], P(('replica', 'tp', 'sub')), parts along dimension 0, may hold values from -0.0625 to 0.0625
- key_cache: bfloat16 [8, 4096, 1024], P('replica', ('tp', 'sub')), parts along dimension 0, may hold values from -240 to 240
- value_cache: bfloat16 [8, 4096, 1024], P('replica', ('tp', 'sub')), parts along dimension 0, may hold values from -6 to 6
- lengths: int32 [8], P('replica'), parts along dimension 0, may hold values from 1 to 4096
- section_order: int32 [32], P('replica'), parts along dimension 0, may hold values from 0 to 15, each once
Outputs:
- mixed_out: bfloat16 [8, 8192], P('replica'), parts along dimension 0
- wqkv_new: bfloat16 [16, 2, 640, 8192], P(('replica', 'tp'), 'sub'), parts along dimension 0
There are 2 independent parts, one for each index of `replica`. A program takes and returns all parts, laid end to end along the dimension named above; each array names one. Nothing has to cross between parts.
Inputs may be any that keep to these rules, and one draw needn't show every extreme that they name: `section_order`: each input row block appears once. The new token's position is lengths[b].
All inputs are finite; a program needn't handle non-finite values.
Results may differ from a plain program's by a relative error of at most 0.0085.
The roundings to bfloat16 on the way count: a program that leaves them out, or rounds other values in their place, can miss the bound.
Values may be sent and summed in bfloat16 or wider, within the bound.
A program may use at most 128 MiB of HBM per device.

v0:
```python
import math
import jax
import jax.numpy as jnp
from jax import lax
from jax.sharding import PartitionSpec as P

HEADS = 64
KV_HEADS = 8
HEAD_DIM = 128
RANKS = 8
ROW_BLOCKS = 16


def passed_along(value, axis, steps):
    count = lax.axis_size(axis)
    pairs = [(source, (source + steps) % count) for source in range(count)]
    return lax.ppermute(value, axis, pairs)


def rotary(values, positions):
    half = values.shape[-1] // 2
    freqs = 500000.0 ** (-jnp.arange(half, dtype=jnp.float32) * 2.0 / values.shape[-1])
    angles = positions.astype(jnp.float32)[:, None] * freqs[None, :]
    cosine = jnp.cos(angles)[:, None, :]
    sine = jnp.sin(angles)[:, None, :]
    first_half = values[..., :half]
    second_half = values[..., half:]
    return jnp.concatenate(
        [first_half * cosine - second_half * sine, second_half * cosine + first_half * sine], -1
    )


def rms_normed(hidden_in, norm_gain):
    widened = hidden_in.astype(jnp.float32)
    factor = lax.rsqrt(jnp.mean(widened * widened, -1, keepdims=True) + 1e-05)
    return (widened, (widened * factor * norm_gain).astype(jnp.bfloat16))


def shards(hidden_in, norm_gain, wqkv_old, wo, key_cache, value_cache, lengths, section_order):
    tp_count = lax.axis_size("tp")
    section_count = tp_count // 4
    per_section = ROW_BLOCKS // section_count
    tp_index = lax.axis_index("tp")
    sub_index = lax.axis_index("sub")
    own_section = tp_index // 4
    device_rank = tp_index * 2 + sub_index
    cols_dev = wqkv_old.shape[2] // section_count
    rows_old = wqkv_old.shape[3]
    block_rows = rows_old // per_section
    old_block = wqkv_old[0, 0].reshape(section_count, cols_dev, rows_old)
    slot_ids = jnp.arange(section_count, dtype=jnp.int32)
    arrived = [lax.dynamic_index_in_dim(old_block, own_section, 0, keepdims=False)]
    for offset in range(1, section_count):
        outgoing = lax.dynamic_index_in_dim(
            old_block, (own_section + offset) % section_count, 0, keepdims=False
        )
        arrived.append(passed_along(outgoing, "tp", 4 * offset))
    received = jnp.stack(arrived, 0)
    sources = (own_section - slot_ids) % section_count
    block_ids = jnp.arange(ROW_BLOCKS, dtype=jnp.int32)
    local_source = (
        sources[:, None] * per_section + jnp.arange(per_section, dtype=jnp.int32)[None, :]
    ).reshape(ROW_BLOCKS)
    target_block = jnp.take(section_order, local_source, axis=0)
    placing = (target_block[None, :] == block_ids[:, None]).astype(jnp.bfloat16)
    received_blocks = jnp.transpose(
        received.reshape(section_count, cols_dev, per_section, block_rows), (0, 2, 1, 3)
    ).reshape(ROW_BLOCKS, cols_dev, block_rows)
    new_weight = jnp.einsum(
        "sa,acr->csr", placing, received_blocks, preferred_element_type=jnp.float32
    ).astype(jnp.bfloat16)
    new_weight = new_weight.reshape(cols_dev, ROW_BLOCKS * block_rows)
    widened, normed = rms_normed(hidden_in, norm_gain)
    projected = lax.dot_general(
        normed, new_weight, (((1,), (1,)), ((), ())), preferred_element_type=jnp.float32
    ).astype(jnp.bfloat16)
    gathered = lax.all_gather(projected[:, None, :], ("tp", "sub"), axis=1, tiled=True)
    seq_count = hidden_in.shape[0]
    projected_all = jnp.transpose(
        gathered.reshape(seq_count, section_count, RANKS, cols_dev), (0, 2, 1, 3)
    ).reshape(seq_count, -1)
    q_width = HEADS * HEAD_DIM
    kv_width = KV_HEADS * HEAD_DIM
    groups = HEADS // KV_HEADS
    queries = rotary(
        projected_all[:, :q_width].astype(jnp.float32).reshape(seq_count, HEADS, HEAD_DIM), lengths
    ).astype(jnp.bfloat16)
    new_keys = rotary(
        projected_all[:, q_width : q_width + kv_width]
        .astype(jnp.float32)
        .reshape(seq_count, KV_HEADS, HEAD_DIM),
        lengths,
    ).astype(jnp.bfloat16)
    new_values = (
        projected_all[:, q_width + kv_width :]
        .astype(jnp.float32)
        .reshape(seq_count, KV_HEADS, HEAD_DIM)
    )
    pos_count = key_cache.shape[1]
    positions = device_rank * pos_count + jnp.arange(pos_count, dtype=jnp.int32)
    usable = (positions[None, :] < lengths[:, None])[:, None, None, :]
    inverse = 1.0 / math.sqrt(HEAD_DIM)
    grouped = queries.reshape(seq_count, KV_HEADS, groups, HEAD_DIM)
    keys_local = key_cache.reshape(seq_count, pos_count, KV_HEADS, HEAD_DIM)
    values_local = value_cache.reshape(seq_count, pos_count, KV_HEADS, HEAD_DIM).astype(jnp.float32)
    scores = (
        jnp.einsum("bkgd,bpkd->bkgp", grouped, keys_local, preferred_element_type=jnp.float32)
        * inverse
    )
    local_top = jnp.max(jnp.where(usable, scores, -1e30), -1)
    weights = jnp.exp(jnp.where(usable, scores - local_top[..., None], -1e30))
    local_sum = jnp.sum(weights, -1).reshape(seq_count, HEADS)
    local_mix = jnp.einsum("bkgp,bpkd->bkgd", weights, values_local).reshape(
        seq_count, HEADS, HEAD_DIM
    )
    local_top = local_top.reshape(seq_count, HEADS)
    heads_dev = wo.shape[0] // HEAD_DIM
    first_head = device_rank * heads_dev
    tops_in, sums_in, mixes_in = (
        lax.all_to_all(local_top[None], ("tp", "sub"), split_axis=2, concat_axis=0, tiled=True),
        lax.all_to_all(local_sum[None], ("tp", "sub"), split_axis=2, concat_axis=0, tiled=True),
        lax.all_to_all(local_mix[None], ("tp", "sub"), split_axis=2, concat_axis=0, tiled=True),
    )
    best = jnp.max(tops_in, 0)
    factors = jnp.exp(tops_in - best[None])
    head_sum = jnp.sum(sums_in * factors, 0)
    head_mix = jnp.sum(mixes_in * factors[..., None], 0)
    own_queries = lax.dynamic_slice_in_dim(queries, first_head, heads_dev, 1).astype(jnp.float32)
    kv_index = (first_head + jnp.arange(heads_dev, dtype=jnp.int32)) // groups
    own_keys = jnp.take(new_keys, kv_index, axis=1).astype(jnp.float32)
    own_values = jnp.take(new_values, kv_index, axis=1)
    own_score = jnp.sum(own_queries * own_keys, -1) * inverse
    highest = jnp.maximum(best, own_score)
    old_scale = jnp.exp(best - highest)
    own_weight = jnp.exp(own_score - highest)
    numerator = head_mix * old_scale[..., None] + own_weight[..., None] * own_values
    denominator = head_sum * old_scale + own_weight
    attended = (
        (numerator / denominator[..., None])
        .reshape(seq_count, heads_dev * HEAD_DIM)
        .astype(jnp.bfloat16)
    )
    partial_out = jnp.dot(attended, wo, preferred_element_type=jnp.float32)
    summed_out = lax.psum(partial_out, ("tp", "sub"))
    mixed_out = (widened + summed_out).astype(jnp.bfloat16)
    return (mixed_out, new_weight[None, None])


def solution(mesh):
    placed = (
        P("replica", None),
        P("replica"),
        P(("replica", "tp"), "sub", None, None),
        P(("replica", "tp", "sub"), None),
        P("replica", ("tp", "sub"), None),
        P("replica", ("tp", "sub"), None),
        P("replica"),
        P("replica"),
    )
    return jax.shard_map(
        shards,
        mesh=mesh,
        in_specs=placed,
        out_specs=(P("replica", None), P(("replica", "tp"), "sub", None, None)),
        check_vma=False,
    )
```

profile of v0, /device:TPU:8, one launch (start us, length us, event | category | flops | bytes accessed | tf_op | source)
XLA Modules:
  0.0 444.4 jit_solution(11691780571699023312)
XLA Ops:
  7.2 9.9 %constant_dynamic-slice_fusion = (bf16[1,640,4096]{2,1,0:T(8,128)(2,1)}, bf16[640,4096]{1,0:T(8,128)(2,1)}) fusion(bf16[2,640,4096]{2,1,0:T(8,128)(2,1)} %bitcast.145, s32[]{:T(128)S(6)} %select_n.109, s32[]{:T(128)S(6)} %select_n.111), kind=kLoop, calls=%fused_computation.104 | loop fusion | bytes 20971528 | tf_op jit(solution)/shard_map/jit(dynamic_index_in_dim)/dynamic_slice | solution.py:52
  17.1 2.6 collective-permute-start
  19.7 0.1 iota_add_fusion
  19.8 0.1 add.183
  19.8 0.1 add.181
  19.9 8.3 %copy.49 = bf16[80,8,8,512]{3,2,1,0:T(8,128)(2,1)} copy(bf16[80,8,8,512]{3,1,2,0:T(8,128)(2,1)} %bitcast.144) | data formatting | bytes 10485760
  28.3 0.7 gather_fusion
  29.1 0.2 fusion.17
  29.3 0.1 broadcast_bitcast_fusion.2
  29.3 0.1 broadcast_compare_fusion
  29.4 0.1 multiply_cosine_fusion
  29.5 215.0 %collective-permute-done = bf16[640,4096]{1,0:T(8,128)(2,1)} collective-permute-done((bf16[640,4096]{1,0:T(8,128)(2,1)}, bf16[640,4096]{1,0:T(8,128)(2,1)}, u32[]{:S(2)}, u32[]{:S(2)}) %collective-permute-start) | collective-permute-done | bytes 5242912 | tf_op jit(solution)/shard_map/ppermute | solution.py:17
  244.5 6.1 %copy.50 = bf16[80,8,8,512]{3,2,1,0:T(8,128)(2,1)S(1)} copy(bf16[80,8,8,512]{3,1,2,0:T(8,128)(2,1)} %bitcast.49) | data formatting | bytes 10485760
  250.7 5.6 %fusion.3 = bf16[640,512,16]{1,2,0:T(8,128)(2,1)} fusion(bf16[1,640,8,512]{3,2,0,1:T(8,128)(2,1)S(1)} %bitcast.149, bf16[1,640,8,512]{3,2,0,1:T(8,128)(2,1)S(1)} %bitcast.148, s32[16]{0:T(128)S(1)} %and_select_fusion.2), kind=kOutput, calls=%fused_computation.7 | convolution fusion | flops 178258176 | bytes 20971584 | tf_op jit(solution)/shard_map/sa,acr->csr/dot_general | solution.py:69
  256.3 20.5 %copy.51 = bf16[80,8,16,512]{3,1,2,0:T(8,128)(2,1)} copy(bf16[80,8,16,512]{3,2,1,0:T(8,128)(2,1)} %bitcast.141) | data formatting | bytes 20971520
  276.8 6.8 %convolution_convert_fusion = bf16[4,640]{1,0:T(4,128)(2,1)S(1)} fusion(bf16[640,8192]{1,0:T(8,128)(2,1)} %bitcast.143, bf16[4,8192]{1,0:T(4,128)(2,1)S(1)} %copy-done.2, f32[8192]{0:T(1024)S(1)} %copy-done.3, f32[4]{0:T(128)S(1)} %add_rsqrt_fusion), kind=kOutput, calls=%fused_computation.17 | convolution fusion | flops 42076672 | bytes 10589200 | tf_op jit(solution)/shard_map/dot_general | solution.py:74
  283.6 19.8 %all-gather = bf16[4,10240]{1,0:T(4,128)(2,1)S(1)} all-gather(bf16[4,640]{1,0:T(4,128)(2,1)S(1)} %convolution_convert_fusion), channel_id=2, replica_groups=mesh['replica'=2,'tp'=8,'sub'=2] {'tp','sub'}, dimensions={1}, use_global_device_ids=true | all-gather | bytes 87040 | tf_op jit(solution)/shard_map/all_gather | solution.py:77
  303.4 0.1 copy.82
  303.6 0.1 subtract_convert_fusion
  303.8 0.8 select_reduce_fusion
  304.6 0.2 fusion.16
  304.8 2.0 fusion.13
  306.8 0.7 copy.45
  307.6 6.6 %all-to-all-start.2 = ((f32[1,4,64]{1,0,2:T(1,128)}), f32[1,4,64]{1,0,2:T(1,128)S(1)}, u32[]{:S(2)}, u32[]{:S(2)}) async-start(f32[1,4,64]{1,0,2:T(1,128)} %bitcast.29), calls=%async_computation.2 | async-start | bytes 65536 | tf_op jit(solution)/shard_map/all_to_all | solution.py:121
  314.2 0.1 subtract_convert_fusion.1
  314.2 0.1 pad_maximum_fusion
  314.3 0.7 copy.37
  315.1 0.6 gather_fusion.1
  315.6 3.6 all-to-all-done.2
  319.3 5.0 %all-to-all-start.1 = ((f32[1,4,64]{1,0,2:T(1,128)}), f32[1,4,64]{1,0,2:T(1,128)S(1)}, u32[]{:S(2)}, u32[]{:S(2)}) async-start(f32[1,4,64]{1,0,2:T(1,128)} %bitcast.16), calls=%async_computation.1 | async-start | bytes 65536 | tf_op jit(solution)/shard_map/all_to_all | solution.py:120
  324.3 0.2 fusion.36
  324.4 0.7 copy.36
  325.2 0.1 copy.40
  325.3 0.6 gather_fusion.2
  325.8 0.2 copy.46
  326.0 3.3 all-to-all-done.1
  329.4 5.0 %all-to-all-start = ((f32[1,4,64,128]{3,1,0,2:T(4,128)}), f32[1,4,64,128]{3,1,0,2:T(4,128)S(1)}, u32[]{:S(2)}, u32[]{:S(2)}) async-start(f32[1,4,64,128]{3,1,0,2:T(4,128)} %copy.36), calls=%async_computation | async-start | bytes 262144 | tf_op jit(solution)/shard_map/all_to_all | solution.py:122
  334.4 0.2 copy.44
  334.7 0.1 broadcast_bitcast_fusion
  334.8 0.2 copy.39
  335.0 0.1 copy.41
  335.1 0.1 broadcast_bitcast_fusion.1
  335.1 4.7 %all-to-all-done = f32[1,4,64,128]{3,1,0,2:T(4,128)S(1)} async-done(((f32[1,4,64,128]{3,1,0,2:T(4,128)}), f32[1,4,64,128]{3,1,0,2:T(4,128)S(1)}, u32[]{:S(2)}, u32[]{:S(2)}) %all-to-all-start) | async-done | bytes 131104 | tf_op jit(solution)/shard_map/all_to_all | solution.py:122
  339.8 0.1 multiply_reduce_fusion
  339.9 5.3 %fusion.41 = f32[4,8192]{1,0:T(4,128)} fusion(bf16[512,8192]{1,0:T(8,128)(2,1)} %param.11, f32[1,4,4,128]{3,2,1,0:T(4,128)S(1)} %broadcast_bitcast_fusion, f32[4,4,128]{2,1,0:T(4,128)S(1)} %gather_fusion.2, f32[1,4,4,128]{3,2,1,0:T(4,128)S(1)} %broadcast_bitcast_fusion.1, f32[4,4,128]{2,0,1:T(4,128)S(1)} %multiply_reduce_fusion, f32[4,4]{0,1:T(4,128)S(1)} %copy.41, ...), kind=kOutput, calls=%fused_computation.69 | convolution fusion | flops 33566720 | bytes 8553024 | tf_op jit(solution)/shard_map/dot_general | solution.py:143
  345.2 16.5 %broadcast_in_dim_reshape.15 = bf16[1,1,640,8192]{3,2,1,0:T(8,128)(2,1)} reshape(bf16[640,16,512]{2,1,0:T(8,128)(2,1)} %bitcast.142) | data formatting | bytes 20971520 | tf_op jit(solution)/shard_map/broadcast_in_dim;reshape | solution.py:146
  361.7 74.2 %all-reduce.2.cloned.1.call-done = f32[4,8192]{1,0:T(4,128)} async-done(((f32[4,8192]{1,0:T(4,128)}), f32[4,8192]{1,0:T(4,128)}) %all-reduce.2.cloned.1.call-update) | async-done | bytes 131088 | tf_op jit(solution)/shard_map/psum | solution.py:144
  435.9 1.6 fusion.20
  (36 shorter events, 0.4 us)
Async XLA Ops:
  7.2 296.6 %copy-start = (bf16[4,256,1024]{2,1,0:T(8,128)(2,1)S(1)}, bf16[4,256,1024]{2,1,0:T(8,128)(2,1)}, u32[]{:S(2)}) copy-start(bf16[4,256,1024]{2,1,0:T(8,128)(2,1)} %param.12) | copy-start | bytes 6291460
  17.1 227.4 %collective-permute-start = (bf16[640,4096]{1,0:T(8,128)(2,1)}, bf16[640,4096]{1,0:T(8,128)(2,1)}, u32[]{:S(2)}, u32[]{:S(2)}) collective-permute-start(bf16[640,4096]{1,0:T(8,128)(2,1)} %get-tuple-element.8), channel_id=1, source_target_pairs={{0,8},{2,10},{4,12},{6,14},{8,0},{10,2},{12,4},{14,6},{1,9},{3,11}... | collective-permute-start | bytes 15728648 | tf_op jit(solution)/shard_map/ppermute | solution.py:17
  19.9 8.4 %copy-start.4 = (s32[4]{0:T(128)S(1)}, s32[4]{0:T(128)}, u32[]{:S(2)}) copy-start(s32[4]{0:T(128)} %param.14) | copy-start | bytes 52
  19.9 8.4 %copy-start.1 = (s32[16]{0:T(128)S(1)}, s32[16]{0:T(128)}, u32[]{:S(2)}) copy-start(s32[16]{0:T(128)} %param.15) | copy-start | bytes 196
  19.9 9.1 %copy-start.2 = (bf16[4,8192]{1,0:T(4,128)(2,1)S(1)}, bf16[4,8192]{1,0:T(4,128)(2,1)}, u32[]{:S(2)}) copy-start(bf16[4,8192]{1,0:T(4,128)(2,1)} %param.8) | copy-start | bytes 196612
  28.3 222.4 %slice-start = ((s8[5242880]{0:T(1024)(128)(4,1)}), s8[1048576]{0:T(1024)(128)(4,1)S(1)}, s32[]{:S(2)}) async-start(s8[5242880]{0:T(1024)(128)(4,1)} %bitcast.146), calls=%async_computation.4 | async-start | bytes 2097152
  244.5 6.1 %slice-start.1 = ((s8[5242880]{0:T(1024)(128)(4,1)}), s8[4194304]{0:T(1024)(128)(4,1)S(1)}, s32[]{:S(2)}) async-start(s8[5242880]{0:T(1024)(128)(4,1)} %bitcast.146), calls=%async_computation.5 | async-start | bytes 8388608
  256.3 20.6 %copy-start.3 = (f32[8192]{0:T(1024)S(1)}, f32[8192]{0:T(1024)}, u32[]{:S(2)}) copy-start(f32[8192]{0:T(1024)} %param.9) | copy-start | bytes 98308
  307.6 11.7 %all-to-all-start.2 = ((f32[1,4,64]{1,0,2:T(1,128)}), f32[1,4,64]{1,0,2:T(1,128)S(1)}, u32[]{:S(2)}, u32[]{:S(2)}) async-start(f32[1,4,64]{1,0,2:T(1,128)} %bitcast.29), calls=%async_computation.2 | async-start | bytes 65536 | tf_op jit(solution)/shard_map/all_to_all | solution.py:121
  319.3 10.1 %all-to-all-start.1 = ((f32[1,4,64]{1,0,2:T(1,128)}), f32[1,4,64]{1,0,2:T(1,128)S(1)}, u32[]{:S(2)}, u32[]{:S(2)}) async-start(f32[1,4,64]{1,0,2:T(1,128)} %bitcast.16), calls=%async_computation.1 | async-start | bytes 65536 | tf_op jit(solution)/shard_map/all_to_all | solution.py:120
  329.4 10.4 %all-to-all-start = ((f32[1,4,64,128]{3,1,0,2:T(4,128)}), f32[1,4,64,128]{3,1,0,2:T(4,128)S(1)}, u32[]{:S(2)}, u32[]{:S(2)}) async-start(f32[1,4,64,128]{3,1,0,2:T(4,128)} %copy.36), calls=%async_computation | async-start | bytes 262144 | tf_op jit(solution)/shard_map/all_to_all | solution.py:122
  334.4 101.6 %all-reduce.2.cloned.1.call-start = ((), (), s32[]{:S(2)}) async-start(), calls=%async_computation.3 | async-start | bytes 262144 | tf_op jit(solution)/shard_map/psum | solution.py:144
Sparse Core Ops, SparseCore 0:
  345.4 90.5 all-reduce.1
where the time goes:
time: 445 us; the launch traced here: 444 us
  waiting for transfers between devices  301 us (68%)
  local copies, waits for them, and re-layouts  66.7 us (15%)
  matrix products  20.4 us (5%)
  blocking collectives  19.8 us (4%)
  starting transfers between devices  19.2 us (4%)
  between operations  14.3 us (3%)
    ppermute x1, waiting for transfers between devices, passed_along(): return lax.ppermute(value, axis, pairs)  215 us
    psum x1, waiting for transfers between devices, shards(): summed_out = lax.psum(partial_out, ('tp', 'sub'))  74.2 us
    unnamed x20, local copies, waits for them, and re-layouts  35.2 us
    all_gather x1, blocking collectives, shards(): lax.all_gather(projected[:, None, :], ('tp', 'sub'), axis=1, tiled=True)  19.8 us
    another operation x1, local copies, waits for them, and re-layouts, shards(): return (mixed_out, new_weight[None, None])  16.5 us
    dynamic_slice x1, local copies, waits for them, and re-layouts, shards(): lax.dynamic_index_in_dim(old_block, own_section, 0, keepdims=False)  9.85 us
  transfers between devices with their start and end apart: 5, of which 5 were waited for; matrix products, arithmetic and copies ran while one was open for 7% of the time, Pallas kernels for 0%

commit v1 on v0

--- a/solution.py
+++ b/solution.py
@@ -141,7 +141,9 @@
         .astype(jnp.bfloat16)
     )
     partial_out = jnp.dot(attended, wo, preferred_element_type=jnp.float32)
-    summed_out = lax.psum(partial_out, ("tp", "sub"))
+    summed_out = partial_out
+    for s in ("sub", "tp"):
+        summed_out = lax.psum(summed_out, s)
     mixed_out = (widened + summed_out).astype(jnp.bfloat16)
     return (mixed_out, new_weight[None, None])
 

time: 445 us -> 449 us (level)
    psum x1 -> x2, waiting for transfers between devices: 74.2 us -> 75.7 us  [shards(): summed_out = lax.psum(summed_out, s)]
  transfers between devices with their start and end apart: 5 -> 6, of which waited for: 5 -> 6; matrix products, arithmetic and copies ran while one was open for 7% -> 7% of each run, Pallas kernels for 0% -> 0%
where the time goes in v1:
time: 449 us; the launch traced here: 446 us
  waiting for transfers between devices  302 us (67%)
  local copies, waits for them, and re-layouts  66.7 us (15%)
  matrix products  20.4 us (5%)
  blocking collectives  19.8 us (4%)
  starting transfers between devices  19.2 us (4%)
  between operations  14.3 us (3%)
    ppermute x1, waiting for transfers between devices, passed_along(): return lax.ppermute(value, axis, pairs)  215 us
    psum x2, waiting for transfers between devices, shards(): summed_out = lax.psum(summed_out, s)  75.7 us
    unnamed x20, local copies, waits for them, and re-layouts  35.2 us
    all_gather x1, blocking collectives, shards(): lax.all_gather(projected[:, None, :], ('tp', 'sub'), axis=1, tiled=True)  19.8 us
    another operation x1, local copies, waits for them, and re-layouts, shards(): return (mixed_out, new_weight[None, None])  16.5 us
    dynamic_slice x1, local copies, waits for them, and re-layouts, shards(): lax.dynamic_index_in_dim(old_block, own_section, 0, keepdims=False)  9.85 us
  transfers between devices with their start and end apart: 6, of which 6 were waited for; matrix products, arithmetic and copies ran while one was open for 7% of the time, Pallas kernels for 0%

profile of v1, /device:TPU:8, one launch (start us, length us, event | category | flops | bytes accessed | tf_op | source)
XLA Modules:
  0.0 445.9 jit_solution(4047615582670502365)
XLA Ops:
  7.2 9.9 %constant_dynamic-slice_fusion = (bf16[1,640,4096]{2,1,0:T(8,128)(2,1)}, bf16[640,4096]{1,0:T(8,128)(2,1)}) fusion(bf16[2,640,4096]{2,1,0:T(8,128)(2,1)} %bitcast.145, s32[]{:T(128)S(6)} %select_n.109, s32[]{:T(128)S(6)} %select_n.111), kind=kLoop, calls=%fused_computation.104 | loop fusion | bytes 20971528 | tf_op jit(solution)/shard_map/jit(dynamic_index_in_dim)/dynamic_slice | solution.py:52
  17.1 2.6 collective-permute-start
  19.7 0.1 iota_add_fusion
  19.8 0.1 add.185
  19.8 0.1 add.183
  19.9 8.3 %copy.49 = bf16[80,8,8,512]{3,2,1,0:T(8,128)(2,1)} copy(bf16[80,8,8,512]{3,1,2,0:T(8,128)(2,1)} %bitcast.144) | data formatting | bytes 10485760
  28.3 0.7 gather_fusion
  29.1 0.2 fusion.17
  29.3 0.1 broadcast_bitcast_fusion.2
  29.3 0.1 broadcast_compare_fusion
  29.4 0.1 multiply_cosine_fusion
  29.5 215.0 %collective-permute-done = bf16[640,4096]{1,0:T(8,128)(2,1)} collective-permute-done((bf16[640,4096]{1,0:T(8,128)(2,1)}, bf16[640,4096]{1,0:T(8,128)(2,1)}, u32[]{:S(2)}, u32[]{:S(2)}) %collective-permute-start) | collective-permute-done | bytes 5242912 | tf_op jit(solution)/shard_map/ppermute | solution.py:17
  244.5 6.1 %copy.50 = bf16[80,8,8,512]{3,2,1,0:T(8,128)(2,1)S(1)} copy(bf16[80,8,8,512]{3,1,2,0:T(8,128)(2,1)} %bitcast.49) | data formatting | bytes 10485760
  250.7 5.6 %fusion.3 = bf16[640,512,16]{1,2,0:T(8,128)(2,1)} fusion(bf16[1,640,8,512]{3,2,0,1:T(8,128)(2,1)S(1)} %bitcast.149, bf16[1,640,8,512]{3,2,0,1:T(8,128)(2,1)S(1)} %bitcast.148, s32[16]{0:T(128)S(1)} %and_select_fusion.2), kind=kOutput, calls=%fused_computation.7 | convolution fusion | flops 178258176 | bytes 20971584 | tf_op jit(solution)/shard_map/sa,acr->csr/dot_general | solution.py:69
  256.3 20.5 %copy.51 = bf16[80,8,16,512]{3,1,2,0:T(8,128)(2,1)} copy(bf16[80,8,16,512]{3,2,1,0:T(8,128)(2,1)} %bitcast.141) | data formatting | bytes 20971520
  276.8 6.8 %convolution_convert_fusion = bf16[4,640]{1,0:T(4,128)(2,1)S(1)} fusion(bf16[640,8192]{1,0:T(8,128)(2,1)} %bitcast.143, bf16[4,8192]{1,0:T(4,128)(2,1)S(1)} %copy-done.2, f32[8192]{0:T(1024)S(1)} %copy-done.3, f32[4]{0:T(128)S(1)} %add_rsqrt_fusion), kind=kOutput, calls=%fused_computation.17 | convolution fusion | flops 42076672 | bytes 10589200 | tf_op jit(solution)/shard_map/dot_general | solution.py:74
  283.6 19.8 %all-gather = bf16[4,10240]{1,0:T(4,128)(2,1)S(1)} all-gather(bf16[4,640]{1,0:T(4,128)(2,1)S(1)} %convolution_convert_fusion), channel_id=2, replica_groups=mesh['replica'=2,'tp'=8,'sub'=2] {'tp','sub'}, dimensions={1}, use_global_device_ids=true | all-gather | bytes 87040 | tf_op jit(solution)/shard_map/all_gather | solution.py:77
  303.6 0.1 subtract_convert_fusion
  303.8 0.8 select_reduce_fusion
  304.6 0.2 fusion.16
  304.8 2.0 fusion.13
  306.8 0.7 copy.45
  307.6 6.6 %all-to-all-start.2 = ((f32[1,4,64]{1,0,2:T(1,128)}), f32[1,4,64]{1,0,2:T(1,128)S(1)}, u32[]{:S(2)}, u32[]{:S(2)}) async-start(f32[1,4,64]{1,0,2:T(1,128)} %bitcast.29), calls=%async_computation.2 | async-start | bytes 65536 | tf_op jit(solution)/shard_map/all_to_all | solution.py:121
  314.2 0.1 subtract_convert_fusion.1
  314.2 0.1 pad_maximum_fusion
  314.3 0.7 copy.37
  315.1 0.6 gather_fusion.1
  315.6 3.6 all-to-all-done.2
  319.3 5.0 %all-to-all-start.1 = ((f32[1,4,64]{1,0,2:T(1,128)}), f32[1,4,64]{1,0,2:T(1,128)S(1)}, u32[]{:S(2)}, u32[]{:S(2)}) async-start(f32[1,4,64]{1,0,2:T(1,128)} %bitcast.16), calls=%async_computation.1 | async-start | bytes 65536 | tf_op jit(solution)/shard_map/all_to_all | solution.py:120
  324.3 0.2 fusion.36
  324.4 0.7 copy.36
  325.2 0.1 copy.40
  325.3 0.6 gather_fusion.2
  325.8 0.2 copy.46
  326.0 3.3 all-to-all-done.1
  329.4 5.0 %all-to-all-start = ((f32[1,4,64,128]{3,1,0,2:T(4,128)}), f32[1,4,64,128]{3,1,0,2:T(4,128)S(1)}, u32[]{:S(2)}, u32[]{:S(2)}) async-start(f32[1,4,64,128]{3,1,0,2:T(4,128)} %copy.36), calls=%async_computation | async-start | bytes 262144 | tf_op jit(solution)/shard_map/all_to_all | solution.py:122
  334.4 0.2 copy.44
  334.7 0.1 broadcast_bitcast_fusion
  334.8 0.2 copy.39
  335.0 0.1 copy.41
  335.1 0.1 broadcast_bitcast_fusion.1
  335.1 4.6 %all-to-all-done = f32[1,4,64,128]{3,1,0,2:T(4,128)S(1)} async-done(((f32[1,4,64,128]{3,1,0,2:T(4,128)}), f32[1,4,64,128]{3,1,0,2:T(4,128)S(1)}, u32[]{:S(2)}, u32[]{:S(2)}) %all-to-all-start) | async-done | bytes 131104 | tf_op jit(solution)/shard_map/all_to_all | solution.py:122
  339.8 0.1 multiply_reduce_fusion
  339.9 5.3 %fusion.41 = f32[4,8192]{1,0:T(4,128)} fusion(bf16[512,8192]{1,0:T(8,128)(2,1)} %param.11, f32[1,4,4,128]{3,2,1,0:T(4,128)S(1)} %broadcast_bitcast_fusion, f32[4,4,128]{2,1,0:T(4,128)S(1)} %gather_fusion.2, f32[1,4,4,128]{3,2,1,0:T(4,128)S(1)} %broadcast_bitcast_fusion.1, f32[4,4,128]{2,0,1:T(4,128)S(1)} %multiply_reduce_fusion, f32[4,4]{0,1:T(4,128)S(1)} %copy.41, ...), kind=kOutput, calls=%fused_computation.69 | convolution fusion | flops 33566720 | bytes 8553024 | tf_op jit(solution)/shard_map/dot_general | solution.py:143
  345.3 18.1 %all-reduce.3.cloned.1.call-done = f32[4,8192]{1,0:T(4,128)} async-done(((f32[4,8192]{1,0:T(4,128)}), f32[4,8192]{1,0:T(4,128)}) %all-reduce.3.cloned.1.call-update) | async-done | bytes 131088 | tf_op jit(solution)/shard_map/psum | solution.py:146
  363.4 16.5 %broadcast_in_dim_reshape.15 = bf16[1,1,640,8192]{3,2,1,0:T(8,128)(2,1)} reshape(bf16[640,16,512]{2,1,0:T(8,128)(2,1)} %bitcast.142) | data formatting | bytes 20971520 | tf_op jit(solution)/shard_map/broadcast_in_dim;reshape | solution.py:148
  379.9 57.6 %all-reduce.5.cloned.1.call-done = f32[4,8192]{1,0:T(4,128)} async-done(((f32[4,8192]{1,0:T(4,128)}), f32[4,8192]{1,0:T(4,128)}) %all-reduce.5.cloned.1.call-update) | async-done | bytes 131088 | tf_op jit(solution)/shard_map/psum | solution.py:146
  437.5 1.6 fusion.20
  (39 shorter events, 0.5 us)
Async XLA Ops:
  7.2 296.6 %copy-start = (bf16[4,256,1024]{2,1,0:T(8,128)(2,1)S(1)}, bf16[4,256,1024]{2,1,0:T(8,128)(2,1)}, u32[]{:S(2)}) copy-start(bf16[4,256,1024]{2,1,0:T(8,128)(2,1)} %param.12) | copy-start | bytes 6291460
  17.1 227.4 %collective-permute-start = (bf16[640,4096]{1,0:T(8,128)(2,1)}, bf16[640,4096]{1,0:T(8,128)(2,1)}, u32[]{:S(2)}, u32[]{:S(2)}) collective-permute-start(bf16[640,4096]{1,0:T(8,128)(2,1)} %get-tuple-element.8), channel_id=1, source_target_pairs={{0,8},{2,10},{4,12},{6,14},{8,0},{10,2},{12,4},{14,6},{1,9},{3,11}... | collective-permute-start | bytes 15728648 | tf_op jit(solution)/shard_map/ppermute | solution.py:17
  19.9 8.4 %copy-start.4 = (s32[4]{0:T(128)S(1)}, s32[4]{0:T(128)}, u32[]{:S(2)}) copy-start(s32[4]{0:T(128)} %param.14) | copy-start | bytes 52
  19.9 8.4 %copy-start.1 = (s32[16]{0:T(128)S(1)}, s32[16]{0:T(128)}, u32[]{:S(2)}) copy-start(s32[16]{0:T(128)} %param.15) | copy-start | bytes 196
  19.9 9.1 %copy-start.2 = (bf16[4,8192]{1,0:T(4,128)(2,1)S(1)}, bf16[4,8192]{1,0:T(4,128)(2,1)}, u32[]{:S(2)}) copy-start(bf16[4,8192]{1,0:T(4,128)(2,1)} %param.8) | copy-start | bytes 196612
  28.3 222.4 %slice-start = ((s8[5242880]{0:T(1024)(128)(4,1)}), s8[1048576]{0:T(1024)(128)(4,1)S(1)}, s32[]{:S(2)}) async-start(s8[5242880]{0:T(1024)(128)(4,1)} %bitcast.146), calls=%async_computation.5 | async-start | bytes 2097152
  244.5 6.1 %slice-start.1 = ((s8[5242880]{0:T(1024)(128)(4,1)}), s8[4194304]{0:T(1024)(128)(4,1)S(1)}, s32[]{:S(2)}) async-start(s8[5242880]{0:T(1024)(128)(4,1)} %bitcast.146), calls=%async_computation.6 | async-start | bytes 8388608
  256.3 20.6 %copy-start.3 = (f32[8192]{0:T(1024)S(1)}, f32[8192]{0:T(1024)}, u32[]{:S(2)}) copy-start(f32[8192]{0:T(1024)} %param.9) | copy-start | bytes 98308
  307.6 11.7 %all-to-all-start.2 = ((f32[1,4,64]{1,0,2:T(1,128)}), f32[1,4,64]{1,0,2:T(1,128)S(1)}, u32[]{:S(2)}, u32[]{:S(2)}) async-start(f32[1,4,64]{1,0,2:T(1,128)} %bitcast.29), calls=%async_computation.2 | async-start | bytes 65536 | tf_op jit(solution)/shard_map/all_to_all | solution.py:121
  319.3 10.1 %all-to-all-start.1 = ((f32[1,4,64]{1,0,2:T(1,128)}), f32[1,4,64]{1,0,2:T(1,128)S(1)}, u32[]{:S(2)}, u32[]{:S(2)}) async-start(f32[1,4,64]{1,0,2:T(1,128)} %bitcast.16), calls=%async_computation.1 | async-start | bytes 65536 | tf_op jit(solution)/shard_map/all_to_all | solution.py:120
  329.4 10.4 %all-to-all-start = ((f32[1,4,64,128]{3,1,0,2:T(4,128)}), f32[1,4,64,128]{3,1,0,2:T(4,128)S(1)}, u32[]{:S(2)}, u32[]{:S(2)}) async-start(f32[1,4,64,128]{3,1,0,2:T(4,128)} %copy.36), calls=%async_computation | async-start | bytes 262144 | tf_op jit(solution)/shard_map/all_to_all | solution.py:122
  334.4 29.0 %all-reduce.3.cloned.1.call-start = ((), (), s32[]{:S(2)}) async-start(), calls=%async_computation.3 | async-start | bytes 262144 | tf_op jit(solution)/shard_map/psum | solution.py:146
  345.2 92.2 %all-reduce.5.cloned.1.call-start = ((), (), s32[]{:S(2)}) async-start(), calls=%async_computation.4 | async-start | bytes 262144 | tf_op jit(solution)/shard_map/psum | solution.py:146
Sparse Core Ops, SparseCore 0:
  345.4 18.0 all-reduce.2
  366.8 70.6 all-reduce.4
